TPU v7x, 32 devices: a whole 2x2x4 slice. The times are simulated.
32 devices in a mesh: gx: 2 (over y), gy: 4 (over x, core), gz: 4 (over z).
Axes of the slice: x: 2, y: 2, z: 4, core: 2. Of those that a mesh axis runs over, the one named last changes fastest.
Arguments:
- right_side: float32 [16, 256, 512], P('gx', 'gy', 'gz'), may hold values from -4 to 4
- start: float32 [16, 256, 512], P('gx', 'gy', 'gz'), may hold values from -6 to 6
Outputs:
- solution: float32 [16, 256, 512], P('gx', 'gy', 'gz')
All inputs are finite; a program needn't handle non-finite values.
Results may differ from a plain program's by a relative error of at most 0.0003.
Values sent between devices are 32-bit elements; how exact they have to be, the bound alone decides.
A program may use at most 128 MiB of HBM per device.

v0:
```python
import functools

import jax
import jax.numpy as jnp
from jax import lax
from jax.experimental import pallas as pl
from jax.experimental.pallas import tpu as pltpu
from jax.sharding import PartitionSpec as P

MESH = pl.DeviceIdType.MESH
SIXTH = 1.0 / 6.0
PAD = 8
DOWN0 = 5
SIDE0 = 4
SIDE1 = 6
RHS1 = 5
CSWEEPS = 8


def dot(a, b):
    return jnp.dot(a, b, precision=lax.Precision.HIGHEST, preferred_element_type=jnp.float32)


def iota(shape, axis):
    return lax.broadcasted_iota(jnp.int32, shape, axis)


def beside(v, edge):
    rows, lanes = v.shape
    up = pltpu.roll(v, 1, axis=0) + pltpu.roll(v, rows - 1, axis=0)
    low = pltpu.roll(v, 1, axis=1)
    high = pltpu.roll(v, lanes - 1, axis=1)
    if edge:
        lane = iota(v.shape, 1)
        low = jnp.where(lane == 0, 0.0, low)
        high = jnp.where(lane == lanes - 1, 0.0, high)
    return up + (low + high)


def update(v_ref, b_ref, code, first, last, origin, colour, factor, edge=False):
    def body(i, carry):
        v = v_ref[i]
        total = (v_ref[i - 1] + v_ref[i + 1]) + beside(v, edge)
        want = lax.rem(i + origin + colour, 2)
        v_ref[i] = jnp.where(code[...] == want, (factor * b_ref[i] + total) * SIXTH, v)
        return carry

    lax.fori_loop(first, last, body, 0)


def residual(v_ref, b_ref, i, factor, edge=False):
    v = v_ref[i]
    total = (v_ref[i - 1] + v_ref[i + 1]) + beside(v, edge)
    return b_ref[i] - (6.0 * v - total) * (1.0 / factor)


class Exchange:
    def __init__(self, ref, sems, send, recv, box, depth, me, sizes):
        self.ref, self.sems, self.send, self.recv = ref, sems, send, recv
        self.c0, self.n, self.rows, self.l0, self.lanes = box
        self.depth, self.me, self.sizes = depth, me, sizes

    def _x(self):
        c0, n, depth = self.c0, self.n, self.depth
        gx = self.sizes[0]
        mx, my, mz = self.me
        rows = pl.ds(PAD, self.rows)
        width = 128
        out = []
        hop = 1
        slot = 0
        while (hop - 1) * n < depth and hop < gx:
            count = min(n, depth - (hop - 1) * n)
            far = (hop - 1) * n
            up = (c0 + n - count, c0 - far - count, mx + hop < gx, mx + hop, mx >= hop)
            down = (c0, c0 + n + far, mx >= hop, mx - hop, mx + hop < gx)
            for src, dst, may_send, peer, may_recv in (up, down):
                copy = pltpu.make_async_remote_copy(
                    src_ref=self.ref.at[pl.ds(src, count), rows, pl.ds(0, width)],
                    dst_ref=self.ref.at[pl.ds(dst, count), rows, pl.ds(0, width)],
                    send_sem=self.sems.at[0, slot],
                    recv_sem=self.sems.at[1, slot],
                    device_id=(peer, my, mz),
                    device_id_type=MESH,
                )
                out.append((copy, may_send, may_recv))
                slot += 1
            hop += 1
        return out

    def _y(self):
        gy = self.sizes[1]
        mx, my, mz = self.me
        planes = pl.ds(self.c0 - self.depth, self.n + 2 * self.depth)
        out = []
        up = (self.rows, 0, my + 1 < gy, my + 1, my >= 1)
        down = (PAD, PAD + self.rows, my >= 1, my - 1, my + 1 < gy)
        for k, (src, dst, may_send, peer, may_recv) in enumerate((up, down)):
            copy = pltpu.make_async_remote_copy(
                src_ref=self.ref.at[planes, pl.ds(src, PAD), pl.ds(0, 128)],
                dst_ref=self.ref.at[planes, pl.ds(dst, PAD), pl.ds(0, 128)],
                send_sem=self.sems.at[0, 4 + k],
                recv_sem=self.sems.at[1, 4 + k],
                device_id=(mx, peer, mz),
                device_id_type=MESH,
            )
            out.append((copy, may_send, may_recv))
        return out

    def _z(self):
        gz = self.sizes[2]
        mx, my, mz = self.me
        out = []
        up = (0, mz + 1 < gz, mz + 1, mz >= 1)
        down = (1, mz >= 1, mz - 1, mz + 1 < gz)
        for k, may_send, peer, may_recv in (up, down):
            copy = pltpu.make_async_remote_copy(
                src_ref=self.send.at[k],
                dst_ref=self.recv.at[k],
                send_sem=self.sems.at[0, 6 + k],
                recv_sem=self.sems.at[1, 6 + k],
                device_id=(mx, my, peer),
                device_id_type=MESH,
            )
            out.append((copy, may_send, may_recv))
        return out

    def _start(self, copies):
        for copy, may_send, may_recv in copies:
            pl.when(may_send)(copy.start)

    def _wait(self, copies):
        for copy, may_send, may_recv in copies:
            pl.when(may_send)(copy.wait_send)
            pl.when(may_recv)(copy.wait_recv)

    def start_x(self):
        self._start(self._x())

    def wait_x(self):
        self._wait(self._x())

    def start_y(self):
        self._start(self._y())

    def wait_y(self):
        self._wait(self._y())

    def _planes(self):
        return range(self.c0 - self.depth, self.c0 + self.n + self.depth)

    def start_z(self):
        d = self.depth
        shape = self.send.shape[1:]
        lane = iota(shape, 1)
        up = jnp.zeros(shape, jnp.float32)
        down = jnp.zeros(shape, jnp.float32)
        for k, i in enumerate(self._planes()):
            v = self.ref[i, :, 0:128]
            here = (lane >= k * d) & (lane < k * d + d)
            up = jnp.where(here, pltpu.roll(v, (k * d - (self.l0 + self.lanes - d)) % 128, axis=1), up)
            down = jnp.where(here, pltpu.roll(v, (k * d - self.l0) % 128, axis=1), down)
        self.send[0] = up
        self.send[1] = down
        self._start(self._z())

    def wait_z(self):
        self._wait(self._z())
        d = self.depth
        gz = self.sizes[2]
        mz = self.me[2]
        shape = self.recv.shape[1:]
        lane = iota(shape, 1)
        low_at = (self.l0 - d) % 128
        high_at = (self.l0 + self.lanes) % 128
        is_low = (lane >= low_at) & (lane < low_at + d)
        is_high = (lane >= high_at) & (lane < high_at + d)
        low_buffer = jnp.where(mz >= 1, self.recv[0], 0.0)
        high_buffer = jnp.where(mz + 1 < gz, self.recv[1], 0.0)
        whole = self.ref.shape[2] == 256
        for k, i in enumerate(self._planes()):
            low = pltpu.roll(low_buffer, (low_at - k * d) % 128, axis=1)
            high = pltpu.roll(high_buffer, (high_at - k * d) % 128, axis=1)
            if whole:
                self.ref[i, :, 128:256] = jnp.where(is_low, low, jnp.where(is_high, high, 0.0))
            else:
                v = self.ref[i]
                self.ref[i] = jnp.where(is_low, low, jnp.where(is_high, high, v))


def kernel(
    sizes, rhs_ref, start_ref, out_ref,
    e0, b0, f0, e1, b1, f1, v2, b2, v3, b3,
    t0, t1, t2, t3, w0, w1, w2, pack, slots,
    za, zb, zc, zd, ze, halo_sems, gather_sems,
):
    gx, gy, gz = sizes
    count = gx * gy * gz
    me = mx, my, mz = lax.axis_index("gx"), lax.axis_index("gy"), lax.axis_index("gz")
    mine = (mx * gy + my) * gz + mz
    lx, ly, lz = rhs_ref.shape
    c0, c1 = DOWN0 + 1, SIDE1 + 2
    hx, hy, hz = lx // 2, ly // 2, lz // 2
    qx, qy, qz = hx // 2, hy // 2, hz // 2
    x2, y2, z2 = gx * qx, gy * qy, gz * qz
    x3, y3, z3 = x2 // 2, y2 // 2, z2 // 2
    z3p = v3.shape[2]
    left = (128 - hz) // 2

    def coords(d):
        return (d // (gy * gz), lax.rem(d // gz, gy), lax.rem(d, gz))

    for ref in (e1, b1, f1, v2, v3):
        ref[...] = jnp.zeros_like(ref)
    rows0 = e0.shape[1]
    for ref in (e0, b0, f0):
        ref[:, 0:PAD, :] = jnp.zeros((ref.shape[0], PAD, 256), jnp.float32)
        ref[:, PAD + ly:, :] = jnp.zeros((ref.shape[0], PAD, 256), jnp.float32)
        for i in list(range(c0)) + list(range(c0 + lx, ref.shape[0])):
            ref[i] = jnp.zeros(ref.shape[1:], jnp.float32)

    barrier = pltpu.get_barrier_semaphore()

    def greet(k, carry):
        d = lax.rem(mine + k, count)
        pl.semaphore_signal(barrier, inc=1, device_id=coords(d), device_id_type=MESH)
        return carry

    lax.fori_loop(1, count, greet, 0)

    e0[c0:c0 + lx, PAD:PAD + ly, 0:128] = start_ref[...]
    b0[c0:c0 + lx, PAD:PAD + ly, 0:128] = rhs_ref[...]

    def code(shape, row0, lane_of, bounds):
        y = iota(shape, 0) + row0
        z = lane_of(iota(shape, 1))
        inside = (y >= 0) & (y < bounds[0]) & (z >= 0) & (z < bounds[1])
        return jnp.where(inside, (y + z) & 1, 5)

    t0[...] = code(t0.shape, my * ly - PAD, lambda c: mz * lz + jnp.where(c < 192, c, c - 256), (gy * ly, gz * lz))
    t1[...] = code(t1.shape, my * hy - PAD, lambda c: mz * hz + c - left, (gy * hy, gz * hz))
    t2[...] = code(t2.shape, -PAD, lambda c: c, (y2, z2))
    t3[...] = code(t3.shape, -PAD, lambda c: c, (y3, z3))

    pl.semaphore_wait(barrier, count - 1)

    box0 = (c0, lx, ly, 0, lz)
    box1 = (c1, hx, hy, left, hz)
    xe0 = Exchange(e0, halo_sems.at[0], za.at[0], za.at[1], box0, DOWN0, me, sizes)
    xb0 = Exchange(b0, halo_sems.at[1], zb.at[0], zb.at[1], box0, DOWN0 - 1, me, sizes)
    xf0 = Exchange(f0, halo_sems.at[2], zc.at[0], zc.at[1], box0, SIDE0, me, sizes)
    xb1 = Exchange(b1, halo_sems.at[3], zd.at[0], zd.at[1], box1, RHS1, me, sizes)
    xf1 = Exchange(f1, halo_sems.at[4], ze.at[0], ze.at[1], box1, SIDE1, me, sizes)

    xe0.start_x()
    xb0.start_x()
    xe0.wait_x()
    xe0.start_y()
    xb0.wait_x()
    xb0.start_y()
    xe0.wait_y()
    xe0.start_z()
    xb0.wait_y()
    xb0.start_z()
    xe0.wait_z()
    xb0.wait_z()

    def span(c, n, depth):
        return (
            jnp.maximum(c - depth, c - mx * n),
            jnp.minimum(c + n + depth, c + (gx - mx) * n),
        )

    for step in range(4):
        first, last = span(c0, lx, 4 - step)
        update(e0, b0, t0, first, last, mx * lx + c0, step % 2, 1.0)

    def pair0(j, carry):
        i = c0 + 2 * j
        r = residual(e0, b0, i, 1.0) + residual(e0, b0, i + 1, 1.0)
        w0[pl.ds(pl.multiple_of(j * ly, 8), ly), :] = r[PAD:PAD + ly, 0:128]
        return carry

    lax.fori_loop(0, hx, pair0, 0)
    r = w0[pl.ds(0, hx * hy, stride=2), :] + w0[pl.ds(1, hx * hy, stride=2), :]
    fold = jnp.where(iota((128, 128), 1) == left + iota((128, 128), 0) // 2, 0.125, 0.0)
    r = dot(r, fold)
    for j in range(hx):
        b1[c1 + j, PAD:PAD + hy, :] = r[j * hy:(j + 1) * hy]

    xb1.start_x()
    f0[c0:c0 + lx, PAD:PAD + ly, 0:128] = e0[c0:c0 + lx, PAD:PAD + ly, 0:128]
    xb1.wait_x()
    xb1.start_y()
    xf0.start_x()
    xb1.wait_y()
    xb1.start_z()
    xf0.wait_x()
    xf0.start_y()
    xb1.wait_z()

    for step in range(4):
        first, last = span(c1, hx, 4 - step)
        update(e1, b1, t1, first, last, mx * hx + c1, step % 2, 4.0)

    for j in range(qx):
        i = c1 + 2 * j
        r = residual(e1, b1, i, 4.0) + residual(e1, b1, i + 1, 4.0)
        w1[j * hy:(j + 1) * hy, :] = r[PAD:PAD + hy]
    r = w1[pl.ds(0, qx * qy, stride=2), :] + w1[pl.ds(1, qx * qy, stride=2), :]
    tiles = qx * qy // 8
    total = None
    for t in range(tiles):
        source = iota((128, 128), 0) - left
        target = iota((128, 128), 1)
        inside = (source >= 0) & (source < hz)
        fold = jnp.where(inside & (target == t * qz + source // 2), 0.125, 0.0)
        part = dot(r[8 * t:8 * t + 8], fold)
        total = part if total is None else total + part
    pack[...] = total
    slots[mine] = total

    def gather(k):
        d = lax.rem(mine + k, count)
        return pltpu.make_async_remote_copy(
            src_ref=pack,
            dst_ref=slots.at[mine],
            send_sem=gather_sems.at[0, d],
            recv_sem=gather_sems.at[1, mine],
            device_id=coords(d),
            device_id_type=MESH,
        )

    def gather_start(k, carry):
        gather(k).start()
        return carry

    lax.fori_loop(1, count, gather_start, 0)

    f1[c1:c1 + hx, PAD:PAD + hy, :] = e1[c1:c1 + hx, PAD:PAD + hy, :]
    xf1.start_x()
    xf0.wait_y()
    xf0.start_z()
    xf1.wait_x()
    xf1.start_y()

    def gather_wait(k, carry):
        d = lax.rem(mine + k, count)
        copy = pltpu.make_async_remote_copy(
            src_ref=pack,
            dst_ref=slots.at[d],
            send_sem=gather_sems.at[0, d],
            recv_sem=gather_sems.at[1, d],
            device_id=coords(d),
            device_id_type=MESH,
        )
        copy.wait_send()
        copy.wait_recv()
        return carry

    lax.fori_loop(1, count, gather_wait, 0)
    xf1.wait_y()
    xf1.start_z()

    per = 128 // qz
    b2[...] = jnp.zeros_like(b2)

    def spread(c, carry):
        cx, cy = c // gy, lax.rem(c, gy)
        lane = iota((8, 128), 1)
        for g in range(gz // per):
            parts = [slots[c * gz + g * per + q] for q in range(per)]
            for t in range(tiles):
                p, h = t // (qy // 8), t % (qy // 8)
                tile = jnp.zeros((8, 128), jnp.float32)
                for q in range(per):
                    here = (lane >= q * qz) & (lane < (q + 1) * qz)
                    tile = jnp.where(here, pltpu.roll(parts[q], ((q - t) * qz) % 128, axis=1), tile)
                rows = pl.ds(pl.multiple_of(PAD + cy * qy + 8 * h, 8), 8)
                b2[1 + cx * qx + p, rows, 128 * g:128 * (g + 1)] = tile
        return carry

    lax.fori_loop(0, gx * gy, spread, 0)

    for step in range(4):
        update(v2, b2, t2, 1, 1 + x2, 1, step % 2, 16.0, True)

    def pair2(q, carry):
        r = residual(v2, b2, 1 + 2 * q, 16.0, True) + residual(v2, b2, 2 + 2 * q, 16.0, True)
        for g in range(z2 // 128):
            w2[g] = r[:, 128 * g:128 * (g + 1)]
        half = y2 // 2
        r = jnp.concatenate(
            [
                w2[g, pl.ds(PAD, half, stride=2), :] + w2[g, pl.ds(PAD + 1, half, stride=2), :]
                for g in range(z2 // 128)
            ],
            axis=1,
        )
        fold = jnp.where(iota((z2, z3p), 1) == iota((z2, z3p), 0) // 2, 0.125, 0.0)
        b3[1 + q, PAD:PAD + half, :] = dot(r, fold)
        return carry

    b3[...] = jnp.zeros_like(b3)
    lax.fori_loop(0, x3, pair2, 0)

    def sweep3(k, carry):
        for colour in (0, 1):
            update(v3, b3, t3, 1, 1 + x3, 1, colour, 64.0, True)
        return carry

    lax.fori_loop(0, CSWEEPS, sweep3, 0)

    def lift3(q, carry):
        half = (y2 + 2 * PAD) // 2
        grow = jnp.where(iota((z3p, z2), 0) == iota((z3p, z2), 1) // 2, 1.0, 0.0)
        v = dot(v3[1 + q, PAD // 2:PAD // 2 + half, :], grow)
        for g in range(z2 // 128):
            w2[g, pl.ds(0, half, stride=2), :] = v[:, 128 * g:128 * (g + 1)]
            w2[g, pl.ds(1, half, stride=2), :] = v[:, 128 * g:128 * (g + 1)]
        for g in range(z2 // 128):
            lanes = slice(128 * g, 128 * (g + 1))
            for i in (1 + 2 * q, 2 + 2 * q):
                v2[i, :, lanes] = v2[i, :, lanes] + w2[g]
        return carry

    lax.fori_loop(0, x3, lift3, 0)

    for step in range(4):
        update(v2, b2, t2, 1, 1 + x2, 1, step % 2, 16.0, True)

    xf1.wait_z()
    rows1 = f1.shape[1]
    grow1 = jnp.where(
        iota((z2, 128), 0) == mz * qz + (iota((z2, 128), 1) - left + 2 * 128) // 2 - 128, 1.0, 0.0
    )
    rows2 = pl.ds(pl.multiple_of(my * qy, 8), rows1 // 2 + PAD)

    def lift2(i, carry):
        q = (mx * hx + i - c1) // 2
        v = dot(v2[1 + q, rows2, :][PAD // 2:PAD // 2 + rows1 // 2], grow1)
        w1[pl.ds(0, rows1 // 2, stride=2), :] = v
        w1[pl.ds(1, rows1 // 2, stride=2), :] = v
        f1[i] = f1[i] + w1[0:rows1, :]
        return carry

    first, last = span(c1, hx, SIDE1)
    lax.fori_loop(first, last, lift2, 0)

    for step in range(4):
        first, last = span(c1, hx, 5 - step)
        update(f1, b1, t1, first, last, mx * hx + c1, step % 2, 4.0)

    xf0.wait_z()
    grow0 = jnp.where(
        iota((128, 256), 0) == (left + iota((128, 256), 1) // 2) % 128, 1.0, 0.0
    )
    half0 = rows0 // 2

    def lift1(j, carry):
        v = dot(f1[j, PAD // 2:PAD // 2 + half0, :], grow0)
        i = c0 + 2 * (j - c1)
        for g in range(2):
            lanes = slice(128 * g, 128 * (g + 1))
            w0[pl.ds(0, half0, stride=2), :] = v[:, lanes]
            w0[pl.ds(1, half0, stride=2), :] = v[:, lanes]
            for k in (i, i + 1):
                f0[k, :, lanes] = f0[k, :, lanes] + w0[0:rows0, :]
        return carry

    first, last = span(c1, hx, SIDE0 // 2)
    lax.fori_loop(first, last, lift1, 0)

    for step in range(4):
        first, last = span(c0, lx, 3 - step)
        update(f0, b0, t0, first, last, mx * lx + c0, step % 2, 1.0)

    out_ref[...] = f0[c0:c0 + lx, PAD:PAD + ly, 0:128]


def local(sizes, right_side, start):
    gx, gy, gz = sizes
    lx, ly, lz = right_side.shape
    c0, c1 = DOWN0 + 1, SIDE1 + 2
    n0, n1 = lx + 2 * c0, lx // 2 + 2 * c1
    r0, r1 = ly + 2 * PAD, ly // 2 + 2 * PAD
    x2, y2, z2 = gx * lx // 4, gy * ly // 4, gz * lz // 4
    x3, y3, z3 = x2 // 2, y2 // 2, z2 // 2
    z3p = -(-z3 // 128) * 128
    f32, i32 = jnp.float32, jnp.int32
    count = gx * gy * gz
    return pl.pallas_call(
        functools.partial(kernel, sizes),
        out_shape=jax.ShapeDtypeStruct(start.shape, f32),
        in_specs=[pl.BlockSpec(memory_space=pltpu.VMEM)] * 2,
        out_specs=pl.BlockSpec(memory_space=pltpu.VMEM),
        scratch_shapes=[
            pltpu.VMEM((n0, r0, 256), f32),
            pltpu.VMEM((n0, r0, 256), f32),
            pltpu.VMEM((n0, r0, 256), f32),
            pltpu.VMEM((n1, r1, 128), f32),
            pltpu.VMEM((n1, r1, 128), f32),
            pltpu.VMEM((n1, r1, 128), f32),
            pltpu.VMEM((x2 + 2, y2 + 2 * PAD, z2), f32),
            pltpu.VMEM((x2 + 2, y2 + 2 * PAD, z2), f32),
            pltpu.VMEM((x3 + 2, y3 + 2 * PAD, z3p), f32),
            pltpu.VMEM((x3 + 2, y3 + 2 * PAD, z3p), f32),
            pltpu.VMEM((r0, 256), i32),
            pltpu.VMEM((r1, 128), i32),
            pltpu.VMEM((y2 + 2 * PAD, z2), i32),
            pltpu.VMEM((y3 + 2 * PAD, z3p), i32),
            pltpu.VMEM((lx // 2 * ly, 128), f32),
            pltpu.VMEM((max(lx // 4 * ly // 2, r1), 128), f32),
            pltpu.VMEM((z2 // 128, y2 + 2 * PAD, 128), f32),
            pltpu.VMEM((8, 128), f32),
            pltpu.VMEM((count, 8, 128), f32),
            pltpu.VMEM((2, 2, r0, 128), f32),
            pltpu.VMEM((2, 2, r0, 128), f32),
            pltpu.VMEM((2, 2, r0, 128), f32),
            pltpu.VMEM((2, 2, r1, 128), f32),
            pltpu.VMEM((2, 2, r1, 128), f32),
            pltpu.SemaphoreType.DMA((5, 2, 8)),
            pltpu.SemaphoreType.DMA((2, count)),
        ],
        compiler_params=pltpu.CompilerParams(
            collective_id=0, has_side_effects=True, vmem_limit_bytes=60 * 1024 * 1024
        ),
    )(right_side, start)


def solution(mesh):
    sizes = (mesh.shape["gx"], mesh.shape["gy"], mesh.shape["gz"])
    spec = P("gx", "gy", "gz")
    return jax.shard_map(
        functools.partial(local, sizes), mesh=mesh, in_specs=(spec, spec), out_specs=spec, check_vma=False
    )
```

profile of v0, /device:TPU:1, one launch (start us, length us, event | category | flops | bytes accessed | tf_op | source)
XLA Modules:
  0.0 70.1 jit_solution(8096486729757906703)
XLA Ops:
  0.0 68.4 %shard_map.28 = f32[8,64,128]{2,1,0:T(8,128)} custom-call(f32[8,64,128]{2,1,0:T(8,128)} %rhs_ref.1, f32[8,64,128]{2,1,0:T(8,128)} %start_ref.1), custom_call_target="tpu_custom_call" | custom-call | tf_op jit(solution)/shard_map/pallas_call | solution.py:492
  68.4 1.7 %copy.4 = f32[8,64,128]{2,1,0:T(8,128)} copy(f32[8,64,128]{2,1,0:T(8,128)} %shard_map.28) | data formatting | bytes 524288
where the time goes:
time: 70.3 us; the launch traced here: 70.1 us
  Pallas kernels  68.4 us (97%)
  local copies, waits for them, and re-layouts  1.67 us (2%)
    pallas_call x1, Pallas kernels, local(): pl.pallas_call(functools.partial(kernel, sizes), out_shape=jax.ShapeDtype...  68.4 us
    unnamed x1, local copies, waits for them, and re-layouts  1.67 us

commit v1 on v0

--- a/solution.py
+++ b/solution.py
@@ -37,15 +37,28 @@
     return up + (low + high)
 
 
-def update(v_ref, b_ref, code, first, last, origin, colour, factor, edge=False):
-    def body(i, carry):
-        v = v_ref[i]
-        total = (v_ref[i - 1] + v_ref[i + 1]) + beside(v, edge)
-        want = lax.rem(i + origin + colour, 2)
-        v_ref[i] = jnp.where(code[...] == want, (factor * b_ref[i] + total) * SIXTH, v)
-        return carry
-
-    lax.fori_loop(first, last, body, 0)
+def update(v_ref, b_ref, code, first, last, origin, colour, factor, edge=False, chunk=4):
+    def some(start, size):
+        planes = [v_ref[start - 1 + k] for k in range(size + 2)]
+        sides = [beside(planes[k + 1], edge) for k in range(size)]
+        fresh = []
+        for k in range(size):
+            total = (planes[k] + planes[k + 2]) + sides[k]
+            want = lax.rem(start + (k + origin + colour), 2)
+            value = (factor * b_ref[start + k] + total) * SIXTH
+            fresh.append(jnp.where(code[...] == want, value, planes[k + 1]))
+        for k in range(size):
+            v_ref[start + k] = fresh[k]
+
+    if isinstance(first, int) and last - first <= chunk:
+        some(first, last - first)
+        return
+
+    def body(c, carry):
+        some(jnp.minimum(first + c * chunk, last - chunk), chunk)
+        return carry
+
+    lax.fori_loop(0, (last - first + chunk - 1) // chunk, body, 0)
 
 
 def residual(v_ref, b_ref, i, factor, edge=False):
@@ -207,8 +220,20 @@
     z3p = v3.shape[2]
     left = (128 - hz) // 2
 
-    def coords(d):
-        return (d // (gy * gz), lax.rem(d // gz, gy), lax.rem(d, gz))
+    def coords(k):
+        steps = (k // (gy * gz), k // gz % gy, k % gz)
+        moved = [at + step for at, step in zip(me, steps)]
+        return tuple(jnp.where(at >= size, at - size, at) for at, size in zip(moved, sizes))
+
+    def number(at):
+        return (at[0] * gy + at[1]) * gz + at[2]
+
+    def others(body):
+        if count <= 64:
+            for k in range(1, count):
+                body(k, 0)
+        else:
+            lax.fori_loop(1, count, body, 0)
 
     for ref in (e1, b1, f1, v2, v3):
         ref[...] = jnp.zeros_like(ref)
@@ -222,11 +247,10 @@
     barrier = pltpu.get_barrier_semaphore()
 
     def greet(k, carry):
-        d = lax.rem(mine + k, count)
-        pl.semaphore_signal(barrier, inc=1, device_id=coords(d), device_id_type=MESH)
-        return carry
-
-    lax.fori_loop(1, count, greet, 0)
+        pl.semaphore_signal(barrier, inc=1, device_id=coords(k), device_id_type=MESH)
+        return carry
+
+    others(greet)
 
     e0[c0:c0 + lx, PAD:PAD + ly, 0:128] = start_ref[...]
     b0[c0:c0 + lx, PAD:PAD + ly, 0:128] = rhs_ref[...]
@@ -278,10 +302,11 @@
     def pair0(j, carry):
         i = c0 + 2 * j
         r = residual(e0, b0, i, 1.0) + residual(e0, b0, i + 1, 1.0)
-        w0[pl.ds(pl.multiple_of(j * ly, 8), ly), :] = r[PAD:PAD + ly, 0:128]
-        return carry
-
-    lax.fori_loop(0, hx, pair0, 0)
+        w0[j * ly:(j + 1) * ly, :] = r[PAD:PAD + ly, 0:128]
+        return carry
+
+    for j in range(hx):
+        pair0(j, 0)
     r = w0[pl.ds(0, hx * hy, stride=2), :] + w0[pl.ds(1, hx * hy, stride=2), :]
     fold = jnp.where(iota((128, 128), 1) == left + iota((128, 128), 0) // 2, 0.125, 0.0)
     r = dot(r, fold)
@@ -295,8 +320,6 @@
     xf0.start_x()
     xb1.wait_y()
     xb1.start_z()
-    xf0.wait_x()
-    xf0.start_y()
     xb1.wait_z()
 
     for step in range(4):
@@ -306,8 +329,10 @@
     for j in range(qx):
         i = c1 + 2 * j
         r = residual(e1, b1, i, 4.0) + residual(e1, b1, i + 1, 4.0)
-        w1[j * hy:(j + 1) * hy, :] = r[PAD:PAD + hy]
-    r = w1[pl.ds(0, qx * qy, stride=2), :] + w1[pl.ds(1, qx * qy, stride=2), :]
+        w1[j, 0:hy, :] = r[PAD:PAD + hy]
+    r = jnp.concatenate(
+        [w1[j, pl.ds(0, qy, stride=2), :] + w1[j, pl.ds(1, qy, stride=2), :] for j in range(qx)], axis=0
+    )
     tiles = qx * qy // 8
     total = None
     for t in range(tiles):
@@ -321,13 +346,14 @@
     slots[mine] = total
 
     def gather(k):
-        d = lax.rem(mine + k, count)
+        at = coords(k)
+        d = number(at)
         return pltpu.make_async_remote_copy(
             src_ref=pack,
             dst_ref=slots.at[mine],
             send_sem=gather_sems.at[0, d],
             recv_sem=gather_sems.at[1, mine],
-            device_id=coords(d),
+            device_id=at,
             device_id_type=MESH,
         )
 
@@ -335,35 +361,34 @@
         gather(k).start()
         return carry
 
-    lax.fori_loop(1, count, gather_start, 0)
+    others(gather_start)
 
     f1[c1:c1 + hx, PAD:PAD + hy, :] = e1[c1:c1 + hx, PAD:PAD + hy, :]
     xf1.start_x()
-    xf0.wait_y()
-    xf0.start_z()
-    xf1.wait_x()
-    xf1.start_y()
+    xf0.wait_x()
+    xf0.start_y()
+    b2[...] = jnp.zeros_like(b2)
+    b3[...] = jnp.zeros_like(b3)
 
     def gather_wait(k, carry):
-        d = lax.rem(mine + k, count)
+        at = coords(k)
+        d = number(at)
         copy = pltpu.make_async_remote_copy(
             src_ref=pack,
             dst_ref=slots.at[d],
             send_sem=gather_sems.at[0, d],
             recv_sem=gather_sems.at[1, d],
-            device_id=coords(d),
+            device_id=at,
             device_id_type=MESH,
         )
         copy.wait_send()
         copy.wait_recv()
         return carry
 
-    lax.fori_loop(1, count, gather_wait, 0)
-    xf1.wait_y()
-    xf1.start_z()
-
+    others(gather_wait)
+    xf1.wait_x()
+    xf1.start_y()
     per = 128 // qz
-    b2[...] = jnp.zeros_like(b2)
 
     def spread(c, carry):
         cx, cy = c // gy, lax.rem(c, gy)
@@ -401,15 +426,30 @@
         b3[1 + q, PAD:PAD + half, :] = dot(r, fold)
         return carry
 
-    b3[...] = jnp.zeros_like(b3)
-    lax.fori_loop(0, x3, pair2, 0)
-
-    def sweep3(k, carry):
+    for q in range(x3):
+        pair2(q, 0)
+    xf0.wait_y()
+    xf0.start_z()
+    xf1.wait_y()
+    xf1.start_z()
+
+    def sweep3(k, planes):
         for colour in (0, 1):
-            update(v3, b3, t3, 1, 1 + x3, 1, colour, 64.0, True)
-        return carry
-
-    lax.fori_loop(0, CSWEEPS, sweep3, 0)
+            now = []
+            for i in range(x3):
+                total = beside(planes[i], True)
+                if i > 0:
+                    total = total + planes[i - 1]
+                if i + 1 < x3:
+                    total = total + planes[i + 1]
+                value = (64.0 * b3[1 + i] + total) * SIXTH
+                now.append(jnp.where(t3[...] == (i + colour) % 2, value, planes[i]))
+            planes = tuple(now)
+        return planes
+
+    planes = lax.fori_loop(0, CSWEEPS, sweep3, tuple(v3[1 + i] for i in range(x3)))
+    for i in range(x3):
+        v3[1 + i] = planes[i]
 
     def lift3(q, carry):
         half = (y2 + 2 * PAD) // 2
@@ -424,7 +464,8 @@
                 v2[i, :, lanes] = v2[i, :, lanes] + w2[g]
         return carry
 
-    lax.fori_loop(0, x3, lift3, 0)
+    for q in range(x3):
+        lift3(q, 0)
 
     for step in range(4):
         update(v2, b2, t2, 1, 1 + x2, 1, step % 2, 16.0, True)
@@ -436,16 +477,20 @@
     )
     rows2 = pl.ds(pl.multiple_of(my * qy, 8), rows1 // 2 + PAD)
 
-    def lift2(i, carry):
-        q = (mx * hx + i - c1) // 2
-        v = dot(v2[1 + q, rows2, :][PAD // 2:PAD // 2 + rows1 // 2], grow1)
-        w1[pl.ds(0, rows1 // 2, stride=2), :] = v
-        w1[pl.ds(1, rows1 // 2, stride=2), :] = v
-        f1[i] = f1[i] + w1[0:rows1, :]
-        return carry
-
-    first, last = span(c1, hx, SIDE1)
-    lax.fori_loop(first, last, lift2, 0)
+    high2 = rows1 // 2 + PAD
+    window = min(x2, qx + 2 * (SIDE1 // 2))
+    begin = jnp.clip(mx * qx - SIDE1 // 2, 0, x2 - window)
+    v = jnp.concatenate([v2[1 + begin + k, rows2, :] for k in range(window)], axis=0)
+    v = dot(v, grow1)
+    for k in range(window):
+        part = v[k * high2:(k + 1) * high2]
+        w1[k, pl.ds(0, high2, stride=2), :] = part
+        w1[k, pl.ds(1, high2, stride=2), :] = part
+    for k in range(window):
+        i = c1 + 2 * (begin + k) - mx * hx
+        lifted = w1[k, PAD:PAD + rows1, :]
+        f1[i] = f1[i] + lifted
+        f1[i + 1] = f1[i + 1] + lifted
 
     for step in range(4):
         first, last = span(c1, hx, 5 - step)
@@ -457,19 +502,27 @@
     )
     half0 = rows0 // 2
 
-    def lift1(j, carry):
-        v = dot(f1[j, PAD // 2:PAD // 2 + half0, :], grow0)
-        i = c0 + 2 * (j - c1)
-        for g in range(2):
-            lanes = slice(128 * g, 128 * (g + 1))
-            w0[pl.ds(0, half0, stride=2), :] = v[:, lanes]
-            w0[pl.ds(1, half0, stride=2), :] = v[:, lanes]
-            for k in (i, i + 1):
-                f0[k, :, lanes] = f0[k, :, lanes] + w0[0:rows0, :]
+    def lift1(c, carry):
+        j = first + 2 * c
+        v = jnp.concatenate([f1[j + k, PAD // 2:PAD // 2 + half0, :] for k in range(2)], axis=0)
+        v = dot(v, grow0)
+        for k in range(2):
+            for g in range(2):
+                at = pl.ds((2 * k + g) * rows0, half0, stride=2)
+                w0[at, :] = v[k * half0:(k + 1) * half0, 128 * g:128 * (g + 1)]
+                at = pl.ds((2 * k + g) * rows0 + 1, half0, stride=2)
+                w0[at, :] = v[k * half0:(k + 1) * half0, 128 * g:128 * (g + 1)]
+        for k in range(2):
+            for g in range(2):
+                lanes = slice(128 * g, 128 * (g + 1))
+                lifted = w0[(2 * k + g) * rows0:(2 * k + g + 1) * rows0, :]
+                for i in range(2):
+                    at = c0 + 2 * (j + k - c1) + i
+                    f0[at, :, lanes] = f0[at, :, lanes] + lifted
         return carry
 
     first, last = span(c1, hx, SIDE0 // 2)
-    lax.fori_loop(first, last, lift1, 0)
+    lax.fori_loop(0, (last - first) // 2, lift1, 0)
 
     for step in range(4):
         first, last = span(c0, lx, 3 - step)
@@ -509,8 +562,8 @@
             pltpu.VMEM((r1, 128), i32),
             pltpu.VMEM((y2 + 2 * PAD, z2), i32),
             pltpu.VMEM((y3 + 2 * PAD, z3p), i32),
-            pltpu.VMEM((lx // 2 * ly, 128), f32),
-            pltpu.VMEM((max(lx // 4 * ly // 2, r1), 128), f32),
+            pltpu.VMEM((max(lx // 2 * ly, 4 * r0), 128), f32),
+            pltpu.VMEM((lx // 4 + SIDE1, r1 + 2 * PAD, 128), f32),
             pltpu.VMEM((z2 // 128, y2 + 2 * PAD, 128), f32),
             pltpu.VMEM((8, 128), f32),
             pltpu.VMEM((count, 8, 128), f32),

time: 70.3 us -> 56.8 us (0.81)
  Pallas kernels: 68.4 us -> 55 us
    pallas_call x1, Pallas kernels: 68.4 us -> 55 us  [local(): pl.pallas_call(functools.partial(kernel, sizes), out_shape=jax.ShapeDtype...]
where the time goes in v1:
time: 56.8 us; the launch traced here: 56.6 us
  Pallas kernels  55 us (97%)
  local copies, waits for them, and re-layouts  1.67 us (3%)
    pallas_call x1, Pallas kernels, local(): pl.pallas_call(functools.partial(kernel, sizes), out_shape=jax.ShapeDtype...  55 us
    unnamed x1, local copies, waits for them, and re-layouts  1.67 us

profile of v1, /device:TPU:1, one launch (start us, length us, event | category | flops | bytes accessed | tf_op | source)
XLA Modules:
  0.0 56.6 jit_solution(17231507240298286813)
XLA Ops:
  0.0 55.0 %shard_map.28 = f32[8,64,128]{2,1,0:T(8,128)} custom-call(f32[8,64,128]{2,1,0:T(8,128)} %rhs_ref.1, f32[8,64,128]{2,1,0:T(8,128)} %start_ref.1), custom_call_target="tpu_custom_call" | custom-call | tf_op jit(solution)/shard_map/pallas_call | solution.py:545
  55.0 1.7 %copy.4 = f32[8,64,128]{2,1,0:T(8,128)} copy(f32[8,64,128]{2,1,0:T(8,128)} %shard_map.28) | data formatting | bytes 524288

commit v2 on v1

--- a/solution.py
+++ b/solution.py
@@ -10,11 +10,14 @@
 MESH = pl.DeviceIdType.MESH
 SIXTH = 1.0 / 6.0
 PAD = 8
+TOP = 16
 DOWN0 = 5
 SIDE0 = 4
 SIDE1 = 6
 RHS1 = 5
 CSWEEPS = 8
+CHUNK0 = 2
+CHUNK1 = 4
 
 
 def dot(a, b):
@@ -67,6 +70,49 @@
     return b_ref[i] - (6.0 * v - total) * (1.0 / factor)
 
 
+def turned(tiles, shift, edge_lane):
+    moved = [pltpu.roll(tile, shift, axis=1) for tile in tiles]
+    if len(moved) == 1:
+        return moved
+    lane = iota(tiles[0].shape, 1)
+    return [jnp.where(lane == edge_lane, moved[1], moved[0]), jnp.where(lane == edge_lane, moved[0], moved[1])]
+
+
+def fine_update(v_ref, b_ref, code, first, last, origin, colour, factor, chunk):
+    tiles, rows = v_ref.shape[1], v_ref.shape[2] - 2 * PAD
+
+    def some(start, size):
+        planes = [[v_ref[start - 1 + k, g, PAD:PAD + rows] for g in range(tiles)] for k in range(size + 2)]
+        fresh = []
+        for k in range(1, size + 1):
+            i = start + (k - 1)
+            low = turned(planes[k], 1, 0)
+            high = turned(planes[k], 127, 127)
+            want = lax.rem(start + (k - 1 + origin + colour), 2)
+            for g in range(tiles):
+                total = v_ref[i, g, PAD - 1:PAD - 1 + rows] + v_ref[i, g, PAD + 1:PAD + 1 + rows]
+                total = (total + (planes[k - 1][g] + planes[k + 1][g])) + (low[g] + high[g])
+                value = (factor * b_ref[i, g, PAD:PAD + rows] + total) * SIXTH
+                fresh.append((i, g, jnp.where(code[g] == want, value, planes[k][g])))
+        for i, g, value in fresh:
+            v_ref[i, g, PAD:PAD + rows] = value
+
+    def body(c, carry):
+        some(jnp.minimum(first + c * chunk, last - chunk), chunk)
+        return carry
+
+    lax.fori_loop(0, (last - first + chunk - 1) // chunk, body, 0)
+
+
+def fine_residual(v_ref, b_ref, i, rows, factor):
+    own = slice(TOP, TOP + rows)
+    tiles = [v_ref[i, g, own] for g in range(v_ref.shape[1])]
+    total = v_ref[i, 0, TOP - 1:TOP - 1 + rows] + v_ref[i, 0, TOP + 1:TOP + 1 + rows]
+    total = total + (v_ref[i - 1, 0, own] + v_ref[i + 1, 0, own])
+    total = total + (turned(tiles, 1, 0)[0] + turned(tiles, 127, 127)[0])
+    return b_ref[i, 0, own] - (6.0 * tiles[0] - total) * (1.0 / factor)
+
+
 class Exchange:
     def __init__(self, ref, sems, send, recv, box, depth, me, sizes):
         self.ref, self.sems, self.send, self.recv = ref, sems, send, recv
@@ -77,8 +123,7 @@
         c0, n, depth = self.c0, self.n, self.depth
         gx = self.sizes[0]
         mx, my, mz = self.me
-        rows = pl.ds(PAD, self.rows)
-        width = 128
+        rows = pl.ds(TOP, self.rows)
         out = []
         hop = 1
         slot = 0
@@ -89,8 +134,8 @@
             down = (c0, c0 + n + far, mx >= hop, mx - hop, mx + hop < gx)
             for src, dst, may_send, peer, may_recv in (up, down):
                 copy = pltpu.make_async_remote_copy(
-                    src_ref=self.ref.at[pl.ds(src, count), rows, pl.ds(0, width)],
-                    dst_ref=self.ref.at[pl.ds(dst, count), rows, pl.ds(0, width)],
+                    src_ref=self.ref.at[pl.ds(src, count), 0, rows],
+                    dst_ref=self.ref.at[pl.ds(dst, count), 0, rows],
                     send_sem=self.sems.at[0, slot],
                     recv_sem=self.sems.at[1, slot],
                     device_id=(peer, my, mz),
@@ -106,12 +151,12 @@
         mx, my, mz = self.me
         planes = pl.ds(self.c0 - self.depth, self.n + 2 * self.depth)
         out = []
-        up = (self.rows, 0, my + 1 < gy, my + 1, my >= 1)
-        down = (PAD, PAD + self.rows, my >= 1, my - 1, my + 1 < gy)
+        up = (TOP + self.rows - PAD, TOP - PAD, my + 1 < gy, my + 1, my >= 1)
+        down = (TOP, TOP + self.rows, my >= 1, my - 1, my + 1 < gy)
         for k, (src, dst, may_send, peer, may_recv) in enumerate((up, down)):
             copy = pltpu.make_async_remote_copy(
-                src_ref=self.ref.at[planes, pl.ds(src, PAD), pl.ds(0, 128)],
-                dst_ref=self.ref.at[planes, pl.ds(dst, PAD), pl.ds(0, 128)],
+                src_ref=self.ref.at[planes, 0, pl.ds(src, PAD)],
+                dst_ref=self.ref.at[planes, 0, pl.ds(dst, PAD)],
                 send_sem=self.sems.at[0, 4 + k],
                 recv_sem=self.sems.at[1, 4 + k],
                 device_id=(mx, peer, mz),
@@ -169,7 +214,7 @@
         up = jnp.zeros(shape, jnp.float32)
         down = jnp.zeros(shape, jnp.float32)
         for k, i in enumerate(self._planes()):
-            v = self.ref[i, :, 0:128]
+            v = self.ref[i, 0, PAD:PAD + shape[0]]
             here = (lane >= k * d) & (lane < k * d + d)
             up = jnp.where(here, pltpu.roll(v, (k * d - (self.l0 + self.lanes - d)) % 128, axis=1), up)
             down = jnp.where(here, pltpu.roll(v, (k * d - self.l0) % 128, axis=1), down)
@@ -190,21 +235,22 @@
         is_high = (lane >= high_at) & (lane < high_at + d)
         low_buffer = jnp.where(mz >= 1, self.recv[0], 0.0)
         high_buffer = jnp.where(mz + 1 < gz, self.recv[1], 0.0)
-        whole = self.ref.shape[2] == 256
+        whole = self.ref.shape[1] == 2
+        rows = slice(PAD, PAD + shape[0])
         for k, i in enumerate(self._planes()):
             low = pltpu.roll(low_buffer, (low_at - k * d) % 128, axis=1)
             high = pltpu.roll(high_buffer, (high_at - k * d) % 128, axis=1)
             if whole:
-                self.ref[i, :, 128:256] = jnp.where(is_low, low, jnp.where(is_high, high, 0.0))
+                self.ref[i, 1, rows] = jnp.where(is_low, low, jnp.where(is_high, high, 0.0))
             else:
-                v = self.ref[i]
-                self.ref[i] = jnp.where(is_low, low, jnp.where(is_high, high, v))
+                v = self.ref[i, 0, rows]
+                self.ref[i, 0, rows] = jnp.where(is_low, low, jnp.where(is_high, high, v))
 
 
 def kernel(
     sizes, rhs_ref, start_ref, out_ref,
     e0, b0, f0, e1, b1, f1, v2, b2, v3, b3,
-    t0, t1, t2, t3, w0, w1, w2, pack, slots,
+    t0, t1, t2, t3, w0, w1, w2, pack, slots, side_send, side_recv,
     za, zb, zc, zd, ze, halo_sems, gather_sems,
 ):
     gx, gy, gz = sizes
@@ -237,11 +283,11 @@
 
     for ref in (e1, b1, f1, v2, v3):
         ref[...] = jnp.zeros_like(ref)
-    rows0 = e0.shape[1]
     for ref in (e0, b0, f0):
-        ref[:, 0:PAD, :] = jnp.zeros((ref.shape[0], PAD, 256), jnp.float32)
-        ref[:, PAD + ly:, :] = jnp.zeros((ref.shape[0], PAD, 256), jnp.float32)
-        for i in list(range(c0)) + list(range(c0 + lx, ref.shape[0])):
+        n0 = ref.shape[0]
+        ref[:, :, 0:TOP] = jnp.zeros((n0, 2, TOP, 128), jnp.float32)
+        ref[:, :, TOP + ly:] = jnp.zeros((n0, 2, TOP, 128), jnp.float32)
+        for i in list(range(c0)) + list(range(c0 + lx, n0)):
             ref[i] = jnp.zeros(ref.shape[1:], jnp.float32)
 
     barrier = pltpu.get_barrier_semaphore()
@@ -252,8 +298,8 @@
 
     others(greet)
 
-    e0[c0:c0 + lx, PAD:PAD + ly, 0:128] = start_ref[...]
-    b0[c0:c0 + lx, PAD:PAD + ly, 0:128] = rhs_ref[...]
+    e0[c0:c0 + lx, 0, TOP:TOP + ly] = start_ref[...]
+    b0[c0:c0 + lx, 0, TOP:TOP + ly] = rhs_ref[...]
 
     def code(shape, row0, lane_of, bounds):
         y = iota(shape, 0) + row0
@@ -261,8 +307,10 @@
         inside = (y >= 0) & (y < bounds[0]) & (z >= 0) & (z < bounds[1])
         return jnp.where(inside, (y + z) & 1, 5)
 
-    t0[...] = code(t0.shape, my * ly - PAD, lambda c: mz * lz + jnp.where(c < 192, c, c - 256), (gy * ly, gz * lz))
-    t1[...] = code(t1.shape, my * hy - PAD, lambda c: mz * hz + c - left, (gy * hy, gz * hz))
+    fine = (gy * ly, gz * lz)
+    t0[0] = code(t0.shape[1:], my * ly - PAD, lambda c: mz * lz + c, fine)
+    t0[1] = code(t0.shape[1:], my * ly - PAD, lambda c: mz * lz + jnp.where(c < 64, c + 128, c - 128), fine)
+    t1[0] = code(t1.shape[1:], my * hy - PAD, lambda c: mz * hz + c - left, (gy * hy, gz * hz))
     t2[...] = code(t2.shape, -PAD, lambda c: c, (y2, z2))
     t3[...] = code(t3.shape, -PAD, lambda c: c, (y3, z3))
 
@@ -276,11 +324,79 @@
     xb1 = Exchange(b1, halo_sems.at[3], zd.at[0], zd.at[1], box1, RHS1, me, sizes)
     xf1 = Exchange(f1, halo_sems.at[4], ze.at[0], ze.at[1], box1, SIDE1, me, sizes)
 
-    xe0.start_x()
-    xb0.start_x()
-    xe0.wait_x()
+    def outer(direction, k):
+        return c0 + lx - k if direction == 0 else c0 + k - 1
+
+    def halo(direction, k):
+        return c0 - k if direction == 0 else c0 + lx + k - 1
+
+    own = slice(TOP, TOP + ly)
+    checks = t0[0, PAD:PAD + ly]
+
+    def black(i):
+        return checks == lax.rem(mx * lx + (i + c0 + 1), 2)
+
+    def merged(ref, direction, k):
+        i = outer(direction, k)
+        return jnp.where(black(i), ref[i, 0, own], ref[outer(direction, k + 1), 0, own])
+
+    peers = ((mx + 1 < gx, mx + 1, mx >= 1), (mx >= 1, mx - 1, mx + 1 < gx))
+
+    def side_copies(planes, group):
+        return [
+            (
+                pltpu.make_async_remote_copy(
+                    src_ref=side_send.at[d, planes],
+                    dst_ref=side_recv.at[d, planes],
+                    send_sem=halo_sems.at[group, 0, d],
+                    recv_sem=halo_sems.at[group, 1, d],
+                    device_id=(peer, my, mz),
+                    device_id_type=MESH,
+                ),
+                may_send,
+                may_recv,
+            )
+            for d, (may_send, peer, may_recv) in enumerate(peers)
+        ]
+
+    near = DOWN0 - 2
+    rhs_copies = [
+        (
+            pltpu.make_async_remote_copy(
+                src_ref=rhs_ref.at[pl.ds((lx - near, 0)[d], near)],
+                dst_ref=b0.at[pl.ds((c0 - near, c0 + lx)[d], near), 0, pl.ds(TOP, ly)],
+                send_sem=halo_sems.at[1, 0, d],
+                recv_sem=halo_sems.at[1, 1, d],
+                device_id=(peer, my, mz),
+                device_id_type=MESH,
+            ),
+            may_send,
+            may_recv,
+        )
+        for d, (may_send, peer, may_recv) in enumerate(peers)
+    ]
+    for copy, may_send, may_recv in rhs_copies:
+        pl.when(may_send)(copy.start)
+    for d in range(2):
+        side_send[d, 0] = merged(e0, d, 1)
+        side_send[d, 1] = merged(e0, d, 3)
+        i = outer(d, 5)
+        moved = pltpu.roll(b0[outer(d, 4), 0, own], 1, axis=0)
+        side_send[d, 2] = jnp.where(black(i), e0[i, 0, own], moved)
+    start_copies = side_copies(pl.ds(0, 3), 0)
+    xe0._start(start_copies)
+    xe0._wait(start_copies)
+    for d in range(2):
+
+        @pl.when(peers[d][2])
+        def _():
+            for k in range(1, 5):
+                e0[halo(d, k), 0, own] = side_recv[d, (k - 1) // 2]
+            e0[halo(d, 5), 0, own] = side_recv[d, 2]
+            b0[halo(d, 4), 0, own] = pltpu.roll(side_recv[d, 2], ly - 1, axis=0)
+
     xe0.start_y()
-    xb0.wait_x()
+    xb0._wait(rhs_copies)
     xb0.start_y()
     xe0.wait_y()
     xe0.start_z()
@@ -297,12 +413,12 @@
 
     for step in range(4):
         first, last = span(c0, lx, 4 - step)
-        update(e0, b0, t0, first, last, mx * lx + c0, step % 2, 1.0)
+        fine_update(e0, b0, t0, first, last, mx * lx + c0, step % 2, 1.0, CHUNK0)
 
     def pair0(j, carry):
         i = c0 + 2 * j
-        r = residual(e0, b0, i, 1.0) + residual(e0, b0, i + 1, 1.0)
-        w0[j * ly:(j + 1) * ly, :] = r[PAD:PAD + ly, 0:128]
+        r = fine_residual(e0, b0, i, ly, 1.0) + fine_residual(e0, b0, i + 1, ly, 1.0)
+        w0[j * ly:(j + 1) * ly, :] = r
         return carry
 
     for j in range(hx):
@@ -311,25 +427,27 @@
     fold = jnp.where(iota((128, 128), 1) == left + iota((128, 128), 0) // 2, 0.125, 0.0)
     r = dot(r, fold)
     for j in range(hx):
-        b1[c1 + j, PAD:PAD + hy, :] = r[j * hy:(j + 1) * hy]
+        b1[c1 + j, 0, TOP:TOP + hy] = r[j * hy:(j + 1) * hy]
 
     xb1.start_x()
-    f0[c0:c0 + lx, PAD:PAD + ly, 0:128] = e0[c0:c0 + lx, PAD:PAD + ly, 0:128]
+    f0[c0:c0 + lx, 0, own] = e0[c0:c0 + lx, 0, own]
+    for d in range(2):
+        side_send[d, 3] = merged(f0, d, 1)
+        side_send[d, 4] = merged(f0, d, 3)
+    side0 = side_copies(pl.ds(3, 2), 2)
     xb1.wait_x()
     xb1.start_y()
-    xf0.start_x()
     xb1.wait_y()
     xb1.start_z()
     xb1.wait_z()
 
     for step in range(4):
         first, last = span(c1, hx, 4 - step)
-        update(e1, b1, t1, first, last, mx * hx + c1, step % 2, 4.0)
+        fine_update(e1, b1, t1, first, last, mx * hx + c1, step % 2, 4.0, CHUNK1)
 
     for j in range(qx):
         i = c1 + 2 * j
-        r = residual(e1, b1, i, 4.0) + residual(e1, b1, i + 1, 4.0)
-        w1[j, 0:hy, :] = r[PAD:PAD + hy]
+        w1[j, 0:hy, :] = fine_residual(e1, b1, i, hy, 4.0) + fine_residual(e1, b1, i + 1, hy, 4.0)
     r = jnp.concatenate(
         [w1[j, pl.ds(0, qy, stride=2), :] + w1[j, pl.ds(1, qy, stride=2), :] for j in range(qx)], axis=0
     )
@@ -363,10 +481,9 @@
 
     others(gather_start)
 
-    f1[c1:c1 + hx, PAD:PAD + hy, :] = e1[c1:c1 + hx, PAD:PAD + hy, :]
+    f1[c1:c1 + hx, 0, TOP:TOP + hy] = e1[c1:c1 + hx, 0, TOP:TOP + hy]
     xf1.start_x()
-    xf0.wait_x()
-    xf0.start_y()
+    xf0._start(side0)
     b2[...] = jnp.zeros_like(b2)
     b3[...] = jnp.zeros_like(b3)
 
@@ -388,6 +505,15 @@
     others(gather_wait)
     xf1.wait_x()
     xf1.start_y()
+    xf0._wait(side0)
+    for d in range(2):
+
+        @pl.when(peers[d][2])
+        def _():
+            for k in range(1, 5):
+                f0[halo(d, k), 0, own] = side_recv[d, 3 + (k - 1) // 2]
+
+    xf0.start_y()
     per = 128 // qz
 
     def spread(c, carry):
@@ -471,13 +597,13 @@
         update(v2, b2, t2, 1, 1 + x2, 1, step % 2, 16.0, True)
 
     xf1.wait_z()
-    rows1 = f1.shape[1]
+    rows1 = f1.shape[2]
     grow1 = jnp.where(
         iota((z2, 128), 0) == mz * qz + (iota((z2, 128), 1) - left + 2 * 128) // 2 - 128, 1.0, 0.0
     )
-    rows2 = pl.ds(pl.multiple_of(my * qy, 8), rows1 // 2 + PAD)
-
-    high2 = rows1 // 2 + PAD
+    rows2 = pl.ds(pl.multiple_of(my * qy, 8), rows1 // 2)
+
+    high2 = rows1 // 2
     window = min(x2, qx + 2 * (SIDE1 // 2))
     begin = jnp.clip(mx * qx - SIDE1 // 2, 0, x2 - window)
     v = jnp.concatenate([v2[1 + begin + k, rows2, :] for k in range(window)], axis=0)
@@ -488,23 +614,25 @@
         w1[k, pl.ds(1, high2, stride=2), :] = part
     for k in range(window):
         i = c1 + 2 * (begin + k) - mx * hx
-        lifted = w1[k, PAD:PAD + rows1, :]
-        f1[i] = f1[i] + lifted
-        f1[i + 1] = f1[i + 1] + lifted
+        rows = slice(PAD, rows1 - PAD)
+        lifted = w1[k, rows, :]
+        f1[i, 0, rows] = f1[i, 0, rows] + lifted
+        f1[i + 1, 0, rows] = f1[i + 1, 0, rows] + lifted
 
     for step in range(4):
         first, last = span(c1, hx, 5 - step)
-        update(f1, b1, t1, first, last, mx * hx + c1, step % 2, 4.0)
+        fine_update(f1, b1, t1, first, last, mx * hx + c1, step % 2, 4.0, CHUNK1)
 
     xf0.wait_z()
     grow0 = jnp.where(
         iota((128, 256), 0) == (left + iota((128, 256), 1) // 2) % 128, 1.0, 0.0
     )
+    rows0 = f0.shape[2]
     half0 = rows0 // 2
 
     def lift1(c, carry):
         j = first + 2 * c
-        v = jnp.concatenate([f1[j + k, PAD // 2:PAD // 2 + half0, :] for k in range(2)], axis=0)
+        v = jnp.concatenate([f1[j + k, 0, PAD:PAD + half0] for k in range(2)], axis=0)
         v = dot(v, grow0)
         for k in range(2):
             for g in range(2):
@@ -514,11 +642,12 @@
                 w0[at, :] = v[k * half0:(k + 1) * half0, 128 * g:128 * (g + 1)]
         for k in range(2):
             for g in range(2):
-                lanes = slice(128 * g, 128 * (g + 1))
-                lifted = w0[(2 * k + g) * rows0:(2 * k + g + 1) * rows0, :]
+                rows = slice(PAD, rows0 - PAD)
+                base = (2 * k + g) * rows0
+                lifted = w0[base + PAD:base + rows0 - PAD, :]
                 for i in range(2):
                     at = c0 + 2 * (j + k - c1) + i
-                    f0[at, :, lanes] = f0[at, :, lanes] + lifted
+                    f0[at, g, rows] = f0[at, g, rows] + lifted
         return carry
 
     first, last = span(c1, hx, SIDE0 // 2)
@@ -526,9 +655,9 @@
 
     for step in range(4):
         first, last = span(c0, lx, 3 - step)
-        update(f0, b0, t0, first, last, mx * lx + c0, step % 2, 1.0)
-
-    out_ref[...] = f0[c0:c0 + lx, PAD:PAD + ly, 0:128]
+        fine_update(f0, b0, t0, first, last, mx * lx + c0, step % 2, 1.0, CHUNK0)
+
+    out_ref[...] = f0[c0:c0 + lx, 0, own]
 
 
 def local(sizes, right_side, start):
@@ -536,7 +665,7 @@
     lx, ly, lz = right_side.shape
     c0, c1 = DOWN0 + 1, SIDE1 + 2
     n0, n1 = lx + 2 * c0, lx // 2 + 2 * c1
-    r0, r1 = ly + 2 * PAD, ly // 2 + 2 * PAD
+    r0, r1 = ly + 2 * TOP, ly // 2 + 2 * TOP
     x2, y2, z2 = gx * lx // 4, gy * ly // 4, gz * lz // 4
     x3, y3, z3 = x2 // 2, y2 // 2, z2 // 2
     z3p = -(-z3 // 128) * 128
@@ -548,30 +677,32 @@
         in_specs=[pl.BlockSpec(memory_space=pltpu.VMEM)] * 2,
         out_specs=pl.BlockSpec(memory_space=pltpu.VMEM),
         scratch_shapes=[
-            pltpu.VMEM((n0, r0, 256), f32),
-            pltpu.VMEM((n0, r0, 256), f32),
-            pltpu.VMEM((n0, r0, 256), f32),
-            pltpu.VMEM((n1, r1, 128), f32),
-            pltpu.VMEM((n1, r1, 128), f32),
-            pltpu.VMEM((n1, r1, 128), f32),
+            pltpu.VMEM((n0, 2, r0, 128), f32),
+            pltpu.VMEM((n0, 2, r0, 128), f32),
+            pltpu.VMEM((n0, 2, r0, 128), f32),
+            pltpu.VMEM((n1, 1, r1, 128), f32),
+            pltpu.VMEM((n1, 1, r1, 128), f32),
+            pltpu.VMEM((n1, 1, r1, 128), f32),
             pltpu.VMEM((x2 + 2, y2 + 2 * PAD, z2), f32),
             pltpu.VMEM((x2 + 2, y2 + 2 * PAD, z2), f32),
             pltpu.VMEM((x3 + 2, y3 + 2 * PAD, z3p), f32),
             pltpu.VMEM((x3 + 2, y3 + 2 * PAD, z3p), f32),
-            pltpu.VMEM((r0, 256), i32),
-            pltpu.VMEM((r1, 128), i32),
+            pltpu.VMEM((2, r0 - 2 * PAD, 128), i32),
+            pltpu.VMEM((1, r1 - 2 * PAD, 128), i32),
             pltpu.VMEM((y2 + 2 * PAD, z2), i32),
             pltpu.VMEM((y3 + 2 * PAD, z3p), i32),
             pltpu.VMEM((max(lx // 2 * ly, 4 * r0), 128), f32),
-            pltpu.VMEM((lx // 4 + SIDE1, r1 + 2 * PAD, 128), f32),
+            pltpu.VMEM((lx // 4 + SIDE1, r1, 128), f32),
             pltpu.VMEM((z2 // 128, y2 + 2 * PAD, 128), f32),
             pltpu.VMEM((8, 128), f32),
             pltpu.VMEM((count, 8, 128), f32),
-            pltpu.VMEM((2, 2, r0, 128), f32),
-            pltpu.VMEM((2, 2, r0, 128), f32),
-            pltpu.VMEM((2, 2, r0, 128), f32),
-            pltpu.VMEM((2, 2, r1, 128), f32),
-            pltpu.VMEM((2, 2, r1, 128), f32),
+            pltpu.VMEM((2, 5, ly, 128), f32),
+            pltpu.VMEM((2, 5, ly, 128), f32),
+            pltpu.VMEM((2, 2, r0 - 2 * PAD, 128), f32),
+            pltpu.VMEM((2, 2, r0 - 2 * PAD, 128), f32),
+            pltpu.VMEM((2, 2, r0 - 2 * PAD, 128), f32),
+            pltpu.VMEM((2, 2, r1 - 2 * PAD, 128), f32),
+            pltpu.VMEM((2, 2, r1 - 2 * PAD, 128), f32),
             pltpu.SemaphoreType.DMA((5, 2, 8)),
             pltpu.SemaphoreType.DMA((2, count)),
         ],

time: 56.8 us -> 55.6 us (0.979)
  Pallas kernels: 55 us -> 53.8 us
    pallas_call x1, Pallas kernels: 55 us -> 53.8 us  [local(): pl.pallas_call(functools.partial(kernel, sizes), out_shape=jax.ShapeDtype...]
where the time goes in v2:
time: 55.6 us; the launch traced here: 55.5 us
  Pallas kernels  53.8 us (97%)
  local copies, waits for them, and re-layouts  1.67 us (3%)
    pallas_call x1, Pallas kernels, local(): pl.pallas_call(functools.partial(kernel, sizes), out_shape=jax.ShapeDtype...  53.8 us
    unnamed x1, local copies, waits for them, and re-layouts  1.67 us

profile of v2, /device:TPU:1, one launch (start us, length us, event | category | flops | bytes accessed | tf_op | source)
XLA Modules:
  0.0 55.5 jit_solution(7031431508626805772)
XLA Ops:
  0.0 53.8 %shard_map.28 = f32[8,64,128]{2,1,0:T(8,128)} custom-call(f32[8,64,128]{2,1,0:T(8,128)} %rhs_ref.1, f32[8,64,128]{2,1,0:T(8,128)} %start_ref.1), custom_call_target="tpu_custom_call" | custom-call | tf_op jit(solution)/shard_map/pallas_call | solution.py:674
  53.8 1.7 %copy.4 = f32[8,64,128]{2,1,0:T(8,128)} copy(f32[8,64,128]{2,1,0:T(8,128)} %shard_map.28) | data formatting | bytes 524288

commit v3 on v2

--- a/solution.py
+++ b/solution.py
@@ -276,12 +276,12 @@
 
     def others(body):
         if count <= 64:
-            for k in range(1, count):
+            for k in reversed(range(1, count)):
                 body(k, 0)
         else:
             lax.fori_loop(1, count, body, 0)
 
-    for ref in (e1, b1, f1, v2, v3):
+    for ref in (b1, f1):
         ref[...] = jnp.zeros_like(ref)
     for ref in (e0, b0, f0):
         n0 = ref.shape[0]
@@ -298,6 +298,8 @@
 
     others(greet)
 
+    for ref in (e1, v2, v3):
+        ref[...] = jnp.zeros_like(ref)
     e0[c0:c0 + lx, 0, TOP:TOP + ly] = start_ref[...]
     b0[c0:c0 + lx, 0, TOP:TOP + ly] = rhs_ref[...]
 

time: 55.6 us -> 55.6 us (level)
  no operation moved by 1% of the time
where the time goes in v3:
time: 55.6 us; the launch traced here: 55.5 us
  Pallas kernels  53.8 us (97%)
  local copies, waits for them, and re-layouts  1.67 us (3%)
    pallas_call x1, Pallas kernels, local(): pl.pallas_call(functools.partial(kernel, sizes), out_shape=jax.ShapeDtype...  53.8 us
    unnamed x1, local copies, waits for them, and re-layouts  1.67 us

profile of v3, /device:TPU:1, one launch (start us, length us, event | category | flops | bytes accessed | tf_op | source)
XLA Modules:
  0.0 55.5 jit_solution(7130060676266179277)
XLA Ops:
  0.0 53.8 %shard_map.28 = f32[8,64,128]{2,1,0:T(8,128)} custom-call(f32[8,64,128]{2,1,0:T(8,128)} %rhs_ref.1, f32[8,64,128]{2,1,0:T(8,128)} %start_ref.1), custom_call_target="tpu_custom_call" | custom-call | tf_op jit(solution)/shard_map/pallas_call | solution.py:676
  53.8 1.7 %copy.4 = f32[8,64,128]{2,1,0:T(8,128)} copy(f32[8,64,128]{2,1,0:T(8,128)} %shard_map.28) | data formatting | bytes 524288
